TPU v7x, 32 devices: a whole 2x2x4 slice. The times are simulated.
32 devices in a mesh: grp: 2 (over x), seq: 16 (over z, y, core).
Axes of the slice: x: 2, y: 2, z: 4, core: 2. Of those that a mesh axis runs over, the one named last changes fastest.
Arguments:
- queries: bfloat16 [256, 4096], P(('grp', 'seq')), parts along dimension 0, may hold values from -9 to 9
- question_keys: bfloat16 [256, 2048], P(('grp', 'seq')), parts along dimension 0, may hold values from -4 to 4
- question_values: bfloat16 [256, 2048], P(('grp', 'seq')), parts along dimension 0, may hold values from -5 to 5
- doc_keys: bfloat16 [16384, 2048], P(('grp', 'seq')), parts along dimension 0, may hold values from -4 to 4
- doc_values: bfloat16 [16384, 2048], P(('grp', 'seq')), parts along dimension 0, may hold values from -5 to 5
- lengths: int32 [2], P('grp'), parts along dimension 0, may hold values from 4 to 128
- offsets: int32 [2], P('grp'), parts along dimension 0, may hold values from 2 to 8192, as said below
Outputs:
- attended: bfloat16 [256, 4096], P(('grp', 'seq')), parts along dimension 0
There are 2 independent parts, one for each index of `grp`. A program takes and returns all parts, laid end to end along the dimension named above; each array names one. Nothing has to cross between parts.
Inputs may be any that keep to these rules, and one draw needn't show every extreme that they name: Some question has offsets equal to 8192.
All inputs are finite; a program needn't handle non-finite values.
Results may differ from a plain program's by a relative error of at most 0.0029.
Values may be sent and summed in bfloat16 or wider, within the bound.
No kernel may reach another device: no remote copies, remote signals or barrier semaphores. Data moves between devices by JAX's collectives and lax.ppermute only.
A program may use at most 64 MiB of HBM per device.

v0:
```python
import math
import jax
import jax.numpy as jnp
from jax import lax
from jax.sharding import PartitionSpec as P

H = 32
KVH = 16
HD = 128
QSCALE = 144
QL = 128
NQ = 1
MASKED = -1e30


def row_tables(start, count, lengths, offsets):
    rows = start + jnp.arange(count, dtype=jnp.int32)
    question = rows // QL
    position = rows % QL
    owner_table = question[:, None] == jnp.arange(NQ, dtype=jnp.int32)[None, :]
    row_length = jnp.sum(jnp.where(owner_table, lengths[None, :], 0), axis=1)
    row_offset = jnp.sum(jnp.where(owner_table, offsets[None, :], 0), axis=1)
    return (question, position, position < row_length, row_offset)


def local(queries, question_keys, question_values, doc_keys, doc_values, lengths, offsets):
    rows_local = queries.shape[0]
    doc_local = doc_keys.shape[0]
    device_count = lax.axis_size("seq")
    device_index = lax.axis_index("seq")
    total_rows = rows_local * device_count
    per_group = H // KVH
    factor_q = QSCALE ** (-0.5)
    key_doc = doc_keys.reshape(doc_local, KVH, HD)
    value_doc = doc_values.reshape(doc_local, KVH, HD)
    key_self = question_keys.reshape(rows_local, KVH, HD)
    value_self = question_values.reshape(rows_local, KVH, HD)
    doc_places = device_index * doc_local + jnp.arange(doc_local, dtype=jnp.int32)
    self_rows = device_index * rows_local + jnp.arange(rows_local, dtype=jnp.int32)
    whole = lax.all_gather(queries, "seq", axis=0, tiled=True)
    block_rows = math.gcd(total_rows, 512)
    block_count = total_rows // block_rows

    def one_block(start):
        piece = whole.reshape(block_rows, KVH, per_group, HD)
        question, position, live_rows, row_offset = row_tables(start, block_rows, lengths, offsets)
        mask_doc = live_rows[:, None] & (doc_places[None, :] < row_offset[:, None])
        mask_self = (
            live_rows[:, None]
            & (self_rows[None, :] // QL == question[:, None])
            & (self_rows[None, :] % QL <= position[:, None])
        )
        mask_doc = mask_doc[:, None, None, :]
        mask_self = mask_self[:, None, None, :]
        scores_doc = (
            jnp.einsum("rgjd,kgd->rgjk", piece, key_doc, preferred_element_type=jnp.float32)
            * factor_q
        )
        scores_self = (
            jnp.einsum("rgjd,kgd->rgjk", piece, key_self, preferred_element_type=jnp.float32)
            * factor_q
        )
        scores_doc = jnp.where(mask_doc, scores_doc, MASKED)
        scores_self = jnp.where(mask_self, scores_self, MASKED)
        block_top = jnp.maximum(jnp.max(scores_doc, axis=-1), jnp.max(scores_self, axis=-1))
        weights_doc = jnp.where(mask_doc, jnp.exp(scores_doc - block_top[..., None]), 0.0).astype(
            jnp.bfloat16
        )
        weights_self = jnp.where(
            mask_self, jnp.exp(scores_self - block_top[..., None]), 0.0
        ).astype(jnp.bfloat16)
        block_den = jnp.sum(weights_doc.astype(jnp.float32), axis=-1) + jnp.sum(
            weights_self.astype(jnp.float32), axis=-1
        )
        block_num = jnp.einsum(
            "rgjk,kgd->rgjd", weights_doc, value_doc, preferred_element_type=jnp.float32
        )
        block_num = block_num + jnp.einsum(
            "rgjk,kgd->rgjd", weights_self, value_self, preferred_element_type=jnp.float32
        )
        return (
            block_num.reshape(block_rows, H * HD),
            block_top.reshape(block_rows, H),
            block_den.reshape(block_rows, H),
        )

    starts = jnp.arange(block_count, dtype=jnp.int32) * block_rows
    numer, row_top, denom = lax.map(one_block, starts)
    numer = numer.reshape(total_rows, H * HD)
    row_top = row_top.reshape(total_rows, H)
    denom = denom.reshape(total_rows, H)
    got_num, got_top, got_den = (
        lax.all_to_all(numer[None], "seq", split_axis=1, concat_axis=0, tiled=True),
        lax.all_to_all(row_top[None], "seq", split_axis=1, concat_axis=0, tiled=True),
        lax.all_to_all(denom[None], "seq", split_axis=1, concat_axis=0, tiled=True),
    )
    overall = jnp.max(got_top, axis=0)
    rescale = jnp.exp(got_top - overall[None])
    total_num = jnp.sum(
        got_num.reshape(device_count, rows_local, H, HD) * rescale[:, :, :, None], axis=0
    )
    total_den = jnp.sum(got_den * rescale, axis=0)
    question, position, live_rows, row_offset = row_tables(
        device_index * rows_local, rows_local, lengths, offsets
    )
    safe_den = jnp.where(live_rows[:, None], total_den, 1.0)
    result = (total_num / safe_den[:, :, None]).reshape(rows_local, H * HD)
    return jnp.where(live_rows[:, None], result, 0.0).astype(jnp.bfloat16)


def solution(mesh):
    placed = (
        P(("grp", "seq"), None),
        P(("grp", "seq"), None),
        P(("grp", "seq"), None),
        P(("grp", "seq"), None),
        P(("grp", "seq"), None),
        P("grp"),
        P("grp"),
    )
    return jax.shard_map(
        local, mesh=mesh, in_specs=placed, out_specs=P(("grp", "seq"), None), check_vma=False
    )
```

profile of v0, /device:TPU:13, one launch (start us, length us, event | category | flops | bytes accessed | tf_op | source)
XLA Modules:
  0.0 149.6 jit_solution(6486073147577093918)
XLA Ops:
  6.5 0.0 copy-start
  6.5 0.0 copy-start.2
  6.5 0.0 all-gather.2.cloned.1.call-start
  6.5 0.7 all-gather.2.cloned.1.call-update
  8.6 3.6 %copy.52 = bf16[64,8,16,128]{3,2,1,0:T(8,128)(2,1)} copy(bf16[64,8,16,128]{3,1,2,0:T(8,128)(2,1)} %bitcast.72) | data formatting | bytes 4194304
  12.1 0.0 copy-done.2
  12.1 0.0 copy-start.4
  12.1 2.5 %copy.50 = bf16[512,2048]{0,1:T(8,128)(2,1)} copy(bf16[512,2048]{1,0:T(8,128)(2,1)S(1)} %copy-done.2) | data formatting | bytes 4194304 | tf_op jit(solution)/shard_map/reshape | solution.py:35
  14.7 0.1 compare_and_fusion.1
  14.8 0.1 compare_and_fusion
  15.0 32.6 %all-gather.2.cloned.1.call-done = bf16[128,4096]{1,0:T(8,128)(2,1)} async-done(((bf16[8,4096]{1,0:T(8,128)(2,1)}), bf16[128,4096]{1,0:T(8,128)(2,1)}) %all-gather.2.cloned.1.call-update) | async-done | bytes 1048592 | tf_op jit(solution)/shard_map/all_gather | solution.py:40
  47.5 1.6 %copy.30 = bf16[128,4096]{0,1:T(8,128)(2,1)S(1)} copy(bf16[128,4096]{1,0:T(8,128)(2,1)} %all-gather.2.cloned.1.call-done) | data formatting | bytes 2097152 | tf_op jit(solution)/shard_map/all_gather | solution.py:40
  49.2 0.0 copy-done.4
  49.2 0.3 fusion.14
  49.4 3.2 %fusion = (f32[128,16,2]{0,2,1:T(2,128)S(1)}, f32[16,512,128,2]{2,1,3,0:T(8,128)S(1)}) fusion(pred[128,512]{0,1:T(8,128)(4,1)S(1)} %compare_and_fusion, bf16[128,16,2,128]{0,3,2,1:T(8,128)(2,1)S(1)} %bitcast.71, bf16[512,16,128,1]{2,1,0,3:T(8,128)(2,1)} %bitcast.74), kind=kOutput, calls=%fused_computation.3 | convolution fusion | flops 543158272 | bytes 11616256 | tf_op jit(solution)/shard_map/while/body/eval_jaxpr/rgjd,kgd->rgjk/dot_general | solution.py:56
  52.6 0.0 copy-start.1
  52.6 0.0 copy-start.3
  52.7 2.1 %convert_reduce_fusion = f32[128,16,2]{0,2,1:T(2,128)S(1)} fusion(f32[128,16,2]{0,2,1:T(2,128)S(1)} %max.18, f32[16,512,128,2]{2,1,3,0:T(8,128)S(1)} %get-tuple-element.32, pred[128,512]{0,1:T(8,128)(4,1)S(1)} %compare_and_fusion), kind=kLoop, calls=%fused_computation.1 | loop fusion | flops 14675968 | bytes 8486912 | tf_op jit(solution)/shard_map/while/body/eval_jaxpr/reduce_sum | solution.py:72
  54.7 1.4 copy-done.1
  56.2 0.1 convert_reduce_fusion.1
  56.3 0.1 copy.39
  56.4 0.6 broadcast.482
  56.9 0.8 reduce.1
  57.7 0.7 reshape.376
  58.4 5.4 %all-to-all-start.2 = ((f32[16,1,256]{2,1,0:T(1,128)}), f32[16,1,256]{2,1,0:T(1,128)S(1)}, u32[]{:S(2)}, u32[]{:S(2)}) async-start(f32[16,1,256]{2,1,0:T(1,128)} %reshape.376), calls=%async_computation.2 | async-start | bytes 32768 | tf_op jit(solution)/shard_map/all_to_all | solution.py:95
  63.8 0.0 copy-done
  63.8 1.8 %fusion.8 = f32[16,128,2,128]{1,3,2,0:T(8,128)} fusion(bf16[8,2048]{1,0:T(8,128)(2,1)S(1)} %copy-done, f32[128,16,2,8]{0,3,2,1:T(8,128)S(1)} %get-tuple-element.34, f32[128,16,2]{0,2,1:T(2,128)S(1)} %max.18, pred[128,8]{0,1:T(8,128)(4,1)S(1)} %compare_and_fusion.1), kind=kOutput, calls=%fused_computation.20 | convolution fusion | flops 8486912 | bytes 2278400 | tf_op jit(solution)/shard_map/while/body/eval_jaxpr/rgjk,kgd->rgjd/dot_general | solution.py:78
  65.6 0.1 copy.37
  65.7 0.8 reduce.3
  66.5 0.7 reshape.374
  67.2 0.8 all-to-all-done.2
  67.9 5.8 %all-to-all-start.1 = ((f32[16,1,256]{2,1,0:T(1,128)}), f32[16,1,256]{2,1,0:T(1,128)S(1)}, u32[]{:S(2)}, u32[]{:S(2)}) async-start(f32[16,1,256]{2,1,0:T(1,128)} %reshape.374), calls=%async_computation.1 | async-start | bytes 32768 | tf_op jit(solution)/shard_map/all_to_all | solution.py:94
  73.7 0.0 copy-done.3
  73.7 7.3 %convolution_add_fusion = f32[16,128,2,128]{1,3,2,0:T(8,128)} fusion(f32[16,128,2,128]{1,3,2,0:T(8,128)} %fusion.8, bf16[512,16,128,1]{0,2,3,1:T(8,128)(2,1)S(1)} %bitcast.73, f32[16,512,128,2]{2,1,3,0:T(8,128)} %copy-done.1, f32[128,16,2]{0,2,1:T(2,128)S(1)} %max.18, pred[128,512]{0,1:T(8,128)(4,1)S(1)} %compare_and_fusion), kind=kOutput, calls=%fused_computation.8 | convolution fusion | flops 547880960 | bytes 14761984 | tf_op jit(solution)/shard_map/while/body/eval_jaxpr/rgjk,kgd->rgjd/dot_general | solution.py:75
  81.0 5.7 %copy.36 = f32[1,128,4096]{2,0,1:T(1,128)} copy(f32[1,128,4096]{1,2,0:T(8,128)} %bitcast.75) | data formatting | bytes 4194304 | tf_op jit(solution)/shard_map/while/body/jit(dynamic_update_index_in_dim)/broadcast_in_dim | solution.py:88
  86.7 0.0 all-to-all-done.1
  86.7 6.1 %all-to-all-start = ((f32[1,128,4096]{2,0,1:T(1,128)}), f32[1,128,4096]{2,0,1:T(1,128)S(1)}, u32[]{:S(2)}, u32[]{:S(2)}) async-start(f32[1,128,4096]{2,0,1:T(1,128)} %copy.36), calls=%async_computation | async-start | bytes 4194304 | tf_op jit(solution)/shard_map/all_to_all | solution.py:93
  92.8 0.7 reduce.2
  93.4 0.1 reshape.377
  93.6 0.7 reduce.4
  94.2 0.1 reshape.375
  94.4 0.1 copy.38
  94.6 0.1 broadcast_select_fusion
  94.6 0.1 copy.40
  94.7 45.4 %all-to-all-done = f32[1,128,4096]{2,0,1:T(1,128)S(1)} async-done(((f32[1,128,4096]{2,0,1:T(1,128)}), f32[1,128,4096]{2,0,1:T(1,128)S(1)}, u32[]{:S(2)}, u32[]{:S(2)}) %all-to-all-start) | async-done | bytes 2097184 | tf_op jit(solution)/shard_map/all_to_all | solution.py:93
  140.2 1.8 %fusion.1 = f32[8,4096]{1,0:T(8,128)S(1)} fusion(f32[1,128,4096]{2,0,1:T(1,128)S(1)} %all-to-all-done, f32[16,8,32]{1,2,0:T(8,128)S(1)} %copy.38), kind=kLoop, calls=%fused_computation.5 | loop fusion | flops 1015808 | bytes 2244608 | tf_op jit(solution)/shard_map/reduce_sum | solution.py:99
  142.0 0.7 fusion.7
  (10 shorter events, 0.1 us)
Async XLA Ops:
  6.5 57.3 %copy-start = (bf16[8,2048]{1,0:T(8,128)(2,1)S(1)}, bf16[8,2048]{1,0:T(8,128)(2,1)}, u32[]{:S(2)}) copy-start(bf16[8,2048]{1,0:T(8,128)(2,1)} %param.9) | copy-start | bytes 98308
  6.5 5.6 %copy-start.2 = (bf16[512,2048]{1,0:T(8,128)(2,1)S(1)}, bf16[512,2048]{1,0:T(8,128)(2,1)}, u32[]{:S(2)}) copy-start(bf16[512,2048]{1,0:T(8,128)(2,1)} %param.11) | copy-start | bytes 6291460
  6.5 41.0 %all-gather.2.cloned.1.call-start = ((), (), s32[]{:S(2)}) async-start(), calls=%async_computation.3 | async-start | bytes 1114112 | tf_op jit(solution)/shard_map/all_gather | solution.py:40
  12.1 37.0 %copy-start.4 = (bf16[8,2048]{1,0:T(8,128)(2,1)S(1)}, bf16[8,2048]{1,0:T(8,128)(2,1)}, u32[]{:S(2)}) copy-start(bf16[8,2048]{1,0:T(8,128)(2,1)} %param.8) | copy-start | bytes 98308
  52.6 3.6 %copy-start.1 = (f32[16,512,128,2]{2,1,3,0:T(8,128)}, f32[16,512,128,2]{2,1,3,0:T(8,128)S(1)}, u32[]{:S(2)}) copy-start(f32[16,512,128,2]{2,1,3,0:T(8,128)S(1)} %get-tuple-element.32) | copy-start | bytes 25165828
  52.6 21.1 %copy-start.3 = (bf16[512,2048]{0,1:T(8,128)(2,1)S(1)}, bf16[512,2048]{0,1:T(8,128)(2,1)}, u32[]{:S(2)}) copy-start(bf16[512,2048]{0,1:T(8,128)(2,1)} %copy.50) | copy-start | bytes 6291460
  58.4 9.5 %all-to-all-start.2 = ((f32[16,1,256]{2,1,0:T(1,128)}), f32[16,1,256]{2,1,0:T(1,128)S(1)}, u32[]{:S(2)}, u32[]{:S(2)}) async-start(f32[16,1,256]{2,1,0:T(1,128)} %reshape.376), calls=%async_computation.2 | async-start | bytes 32768 | tf_op jit(solution)/shard_map/all_to_all | solution.py:95
  67.9 18.7 %all-to-all-start.1 = ((f32[16,1,256]{2,1,0:T(1,128)}), f32[16,1,256]{2,1,0:T(1,128)S(1)}, u32[]{:S(2)}, u32[]{:S(2)}) async-start(f32[16,1,256]{2,1,0:T(1,128)} %reshape.374), calls=%async_computation.1 | async-start | bytes 32768 | tf_op jit(solution)/shard_map/all_to_all | solution.py:94
  86.7 53.5 %all-to-all-start = ((f32[1,128,4096]{2,0,1:T(1,128)}), f32[1,128,4096]{2,0,1:T(1,128)S(1)}, u32[]{:S(2)}, u32[]{:S(2)}) async-start(f32[1,128,4096]{2,0,1:T(1,128)} %copy.36), calls=%async_computation | async-start | bytes 4194304 | tf_op jit(solution)/shard_map/all_to_all | solution.py:93
Sparse Core Ops, SparseCore 0:
  9.5 38.0 all-gather.1
where the time goes:
time: 150 us
  waiting for transfers between devices  79.5 us (53%)
  local copies, waits for them, and re-layouts  17.5 us (12%)
  starting transfers between devices  17.2 us (11%)
  between operations  14.9 us (10%)
  matrix products  12.5 us (8%)
  other arithmetic  7.99 us (5%)
    all_to_all x1, waiting for transfers between devices, local(): lax.all_to_all(numer[None], 'seq', split_axis=1, concat_axis=0, tiled=True)  45.4 us
    all_gather x1, waiting for transfers between devices, local(): whole = lax.all_gather(queries, 'seq', axis=0, tiled=True)  32.6 us
    dot_general x1, matrix products, one_block(): jnp.einsum('rgjk,kgd->rgjd', weights_doc, value_doc, preferred_element_ty...  7.29 us
    unnamed x16, local copies, waits for them, and re-layouts  7.29 us
    all_to_all x1, starting transfers between devices, local(): lax.all_to_all(numer[None], 'seq', split_axis=1, concat_axis=0, tiled=True)  6.06 us
    all_to_all x1, starting transfers between devices, local(): lax.all_to_all(row_top[None], 'seq', split_axis=1, concat_axis=0, tiled=T...  5.76 us
    broadcast_in_dim x1, local copies, waits for them, and re-layouts, local(): numer, row_top, denom = lax.map(one_block, starts)  5.68 us
    all_to_all x1, starting transfers between devices, local(): lax.all_to_all(denom[None], 'seq', split_axis=1, concat_axis=0, tiled=True)  5.37 us
  transfers between devices with their start and end apart: 4, of which 3 were waited for; matrix products, arithmetic and copies ran while one was open for 16% of the time, Pallas kernels for 0%

commit v1 on v0

--- a/solution.py
+++ b/solution.py
@@ -90,7 +90,15 @@
     row_top = row_top.reshape(total_rows, H)
     denom = denom.reshape(total_rows, H)
     got_num, got_top, got_den = (
-        lax.all_to_all(numer[None], "seq", split_axis=1, concat_axis=0, tiled=True),
+        jnp.concatenate(
+            lax.all_to_all(
+                jnp.stack(jnp.split(numer[None], lax.axis_size("seq"), axis=1)),
+                "seq",
+                split_axis=0,
+                concat_axis=0,
+            ),
+            0,
+        ),
         lax.all_to_all(row_top[None], "seq", split_axis=1, concat_axis=0, tiled=True),
         lax.all_to_all(denom[None], "seq", split_axis=1, concat_axis=0, tiled=True),
     )

time: 150 us -> 206 us (1.37)
  local copies, waits for them, and re-layouts: 17.5 us -> 76.3 us
  matrix products: 12.5 us -> 7.81 us
  waiting for transfers between devices: 79.5 us -> 82 us
    unnamed x16 -> x49, local copies, waits for them, and re-layouts: 7.29 us -> 57.7 us
    split x0 -> x1, local copies, waits for them, and re-layouts: none -> 13.3 us  [local(): jnp.split(numer[None], lax.axis_size('seq'), axis=1)]
    broadcast_in_dim x1 -> x0, local copies, waits for them, and re-layouts: 5.68 us -> none  [local(): numer, row_top, denom = lax.map(one_block, starts)]
    all_to_all x1, waiting for transfers between devices: 0.01 us -> 3.48 us  [local(): lax.all_to_all(row_top[None], 'seq', split_axis=1, concat_axis=0, tiled=T...]
  transfers between devices with their start and end apart: 4 -> 4, of which waited for: 3 -> 3; matrix products, arithmetic and copies ran while one was open for 16% -> 39% of each run, Pallas kernels for 0% -> 0%
where the time goes in v1:
time: 206 us; the launch traced here: 205 us
  waiting for transfers between devices  82 us (40%)
  local copies, waits for them, and re-layouts  76.3 us (37%)
  starting transfers between devices  17.4 us (8%)
  between operations  14.9 us (7%)
  matrix products  7.81 us (4%)
  other arithmetic  6.94 us (3%)
    unnamed x49, local copies, waits for them, and re-layouts  57.7 us
    all_to_all x1, waiting for transfers between devices, local(): lax.all_to_all(jnp.stack(jnp.split(numer[None], lax.axis_size('seq'), axi...  45.4 us
    all_gather x1, waiting for transfers between devices, local(): whole = lax.all_gather(queries, 'seq', axis=0, tiled=True)  32.4 us
    split x1, local copies, waits for them, and re-layouts, local(): jnp.split(numer[None], lax.axis_size('seq'), axis=1)  13.3 us
    all_to_all x1, starting transfers between devices, local(): lax.all_to_all(row_top[None], 'seq', split_axis=1, concat_axis=0, tiled=T...  6.03 us
    all_to_all x1, starting transfers between devices, local(): lax.all_to_all(jnp.stack(jnp.split(numer[None], lax.axis_size('seq'), axi...  6 us
    dot_general x1, matrix products, one_block(): jnp.einsum('rgjk,kgd->rgjd', weights_doc, value_doc, preferred_element_ty...  5.48 us
    all_to_all x1, starting transfers between devices, local(): lax.all_to_all(denom[None], 'seq', split_axis=1, concat_axis=0, tiled=True)  5.37 us
  transfers between devices with their start and end apart: 4, of which 3 were waited for; matrix products, arithmetic and copies ran while one was open for 39% of the time, Pallas kernels for 0%

profile of v1, /device:TPU:13, one launch (start us, length us, event | category | flops | bytes accessed | tf_op | source)
XLA Modules:
  0.0 205.3 jit_solution(3214430472673109701)
XLA Ops:
  6.5 0.7 all-gather.2.cloned.1.call-update
  8.6 3.7 %copy.112 = bf16[64,8,16,128]{3,2,1,0:T(8,128)(2,1)} copy(bf16[64,8,16,128]{3,1,2,0:T(8,128)(2,1)} %bitcast.103) | data formatting | bytes 4194304
  12.3 2.5 %copy.94 = bf16[512,2048]{0,1:T(8,128)(2,1)} copy(bf16[512,2048]{1,0:T(8,128)(2,1)S(1)} %copy-done.2) | data formatting | bytes 4194304 | tf_op jit(solution)/shard_map/reshape | solution.py:35
  15.0 0.1 compare_and_fusion
  15.1 32.4 %all-gather.2.cloned.1.call-done = bf16[128,4096]{1,0:T(8,128)(2,1)} async-done(((bf16[8,4096]{1,0:T(8,128)(2,1)}), bf16[128,4096]{1,0:T(8,128)(2,1)}) %all-gather.2.cloned.1.call-update) | async-done | bytes 1048592 | tf_op jit(solution)/shard_map/all_gather | solution.py:40
  47.5 1.6 copy.57
  49.2 0.3 fusion.15
  49.5 1.6 fusion
  51.1 2.1 %convert_reduce_fusion = f32[128,16,2]{0,2,1:T(2,128)S(1)} fusion(f32[128,16,2]{0,2,1:T(2,128)S(1)} %max.18, f32[16,512,128,2]{2,1,3,0:T(8,128)S(1)} %get-tuple-element.63, pred[128,512]{0,1:T(8,128)(4,1)S(1)} %compare_and_fusion), kind=kLoop, calls=%fused_computation.1 | loop fusion | flops 14675968 | bytes 8486912 | tf_op jit(solution)/shard_map/while/body/eval_jaxpr/reduce_sum | solution.py:72
  53.1 1.1 copy-done.1
  54.3 0.1 copy.82
  54.4 0.6 broadcast.482
  55.0 0.8 reduce.1
  55.8 0.7 reshape.354
  56.5 5.4 %all-to-all-start.2 = ((f32[16,1,256]{2,1,0:T(1,128)}), f32[16,1,256]{2,1,0:T(1,128)S(1)}, u32[]{:S(2)}, u32[]{:S(2)}) async-start(f32[16,1,256]{2,1,0:T(1,128)} %reshape.354), calls=%async_computation.2 | async-start | bytes 32768 | tf_op jit(solution)/shard_map/all_to_all | solution.py:103
  61.9 0.5 fusion.8
  62.4 5.5 %convolution_add_fusion = f32[16,128,2,128]{1,3,2,0:T(8,128)S(1)} fusion(f32[16,128,2,128]{1,3,2,0:T(8,128)S(1)} %fusion.8, bf16[512,16,128,1]{0,2,3,1:T(8,128)(2,1)S(1)} %bitcast.104, f32[16,512,128,2]{2,1,3,0:T(8,128)} %copy-done.1, f32[128,16,2]{0,2,1:T(2,128)S(1)} %max.18, pred[128,512]{0,1:T(8,128)(4,1)S(1)} %compare_and_fusion), kind=kOutput, calls=%fused_computation.8 | convolution fusion | flops 547880960 | bytes 14761984 | tf_op jit(solution)/shard_map/while/body/eval_jaxpr/rgjk,kgd->rgjd/dot_general | solution.py:75
  67.9 13.3 %fusion.14 = (f32[1,8,4096]{1,2,0:T(8,128)S(1)}, f32[1,8,4096]{1,2,0:T(8,128)}, f32[1,8,4096]{1,2,0:T(8,128)}, f32[1,8,4096]{1,2,0:T(8,128)}, f32[1,8,4096]{1,2,...) fusion(f32[1,128,4096]{1,2,0:T(8,128)S(1)} %bitcast.100), kind=kLoop, calls=%fused_computation.59 | loop fusion | bytes 4194304 | tf_op jit(solution)/shard_map/split | solution.py:95
  81.2 2.2 %copy.110 = f32[1,8,4096]{2,1,0:T(8,128)S(1)} copy(f32[1,8,4096]{1,2,0:T(8,128)} %get-tuple-element.32) | data formatting | bytes 262144
  83.3 2.2 %copy.109 = f32[1,8,4096]{2,1,0:T(8,128)S(1)} copy(f32[1,8,4096]{1,2,0:T(8,128)} %get-tuple-element.33) | data formatting | bytes 262144
  85.5 2.2 %copy.108 = f32[1,8,4096]{2,1,0:T(8,128)S(1)} copy(f32[1,8,4096]{1,2,0:T(8,128)} %get-tuple-element.34) | data formatting | bytes 262144
  87.7 2.2 %copy.107 = f32[1,8,4096]{2,1,0:T(8,128)S(1)} copy(f32[1,8,4096]{1,2,0:T(8,128)} %get-tuple-element.35) | data formatting | bytes 262144
  89.8 2.2 %copy.106 = f32[1,8,4096]{2,1,0:T(8,128)S(1)} copy(f32[1,8,4096]{1,2,0:T(8,128)} %get-tuple-element.36) | data formatting | bytes 262144
  92.0 2.2 %copy.105 = f32[1,8,4096]{2,1,0:T(8,128)S(1)} copy(f32[1,8,4096]{1,2,0:T(8,128)} %get-tuple-element.37) | data formatting | bytes 262144
  94.2 2.2 %copy.104 = f32[1,8,4096]{2,1,0:T(8,128)S(1)} copy(f32[1,8,4096]{1,2,0:T(8,128)} %get-tuple-element.38) | data formatting | bytes 262144
  96.3 2.2 %copy.103 = f32[1,8,4096]{2,1,0:T(8,128)S(1)} copy(f32[1,8,4096]{1,2,0:T(8,128)} %get-tuple-element.52) | data formatting | bytes 262144
  98.5 2.2 %copy.102 = f32[1,8,4096]{2,1,0:T(8,128)S(1)} copy(f32[1,8,4096]{1,2,0:T(8,128)} %get-tuple-element.54) | data formatting | bytes 262144
  100.7 2.2 %copy.101 = f32[1,8,4096]{2,1,0:T(8,128)S(1)} copy(f32[1,8,4096]{1,2,0:T(8,128)} %get-tuple-element.56) | data formatting | bytes 262144
  102.8 2.8 %copy.100 = f32[1,8,4096]{2,1,0:T(8,128)} copy(f32[1,8,4096]{1,2,0:T(8,128)} %get-tuple-element.57) | data formatting | bytes 262144
  105.7 2.8 %copy.99 = f32[1,8,4096]{2,1,0:T(8,128)} copy(f32[1,8,4096]{1,2,0:T(8,128)} %get-tuple-element.58) | data formatting | bytes 262144
  108.5 2.8 %copy.98 = f32[1,8,4096]{2,1,0:T(8,128)} copy(f32[1,8,4096]{1,2,0:T(8,128)} %get-tuple-element.59) | data formatting | bytes 262144
  111.3 2.8 %copy.97 = f32[1,8,4096]{2,1,0:T(8,128)} copy(f32[1,8,4096]{1,2,0:T(8,128)} %get-tuple-element.60) | data formatting | bytes 262144
  114.1 2.8 %copy.96 = f32[1,8,4096]{2,1,0:T(8,128)} copy(f32[1,8,4096]{1,2,0:T(8,128)} %get-tuple-element.61) | data formatting | bytes 262144
  116.9 1.5 bitcast_dynamic-update-slice_fusion.15
  118.4 1.6 bitcast_dynamic-update-slice_fusion.14
  120.0 1.6 bitcast_dynamic-update-slice_fusion.13
  121.6 1.6 bitcast_dynamic-update-slice_fusion.12
  123.1 1.6 bitcast_dynamic-update-slice_fusion.11
  124.7 0.6 bitcast_dynamic-update-slice_fusion.10
  125.3 0.7 bitcast_dynamic-update-slice_fusion.9
  126.0 0.7 bitcast_dynamic-update-slice_fusion.8
  126.7 0.7 bitcast_dynamic-update-slice_fusion.7
  127.3 0.7 bitcast_dynamic-update-slice_fusion.6
  128.0 0.7 bitcast_dynamic-update-slice_fusion.5
  128.6 0.7 bitcast_dynamic-update-slice_fusion.4
  129.3 0.7 bitcast_dynamic-update-slice_fusion.3
  130.0 0.7 bitcast_dynamic-update-slice_fusion.2
  130.6 0.6 bitcast_dynamic-update-slice_fusion.1
  131.3 0.1 copy.79
  131.4 0.8 reduce.3
  132.2 0.7 reshape.352
  132.9 0.6 copy.111
  133.4 6.0 %all-to-all-start.1 = ((f32[16,1,256]{2,1,0:T(1,128)}), f32[16,1,256]{2,1,0:T(1,128)S(1)}, u32[]{:S(2)}, u32[]{:S(2)}) async-start(f32[16,1,256]{2,1,0:T(1,128)} %reshape.352), calls=%async_computation.1 | async-start | bytes 32768 | tf_op jit(solution)/shard_map/all_to_all | solution.py:102
  139.5 0.7 bitcast_dynamic-update-slice_fusion
  140.1 3.5 %all-to-all-done.1 = f32[16,1,256]{2,1,0:T(1,128)S(1)} async-done(((f32[16,1,256]{2,1,0:T(1,128)}), f32[16,1,256]{2,1,0:T(1,128)S(1)}, u32[]{:S(2)}, u32[]{:S(2)}) %all-to-all-start.1) | async-done | bytes 16416 | tf_op jit(solution)/shard_map/all_to_all | solution.py:102
  143.6 6.0 %all-to-all-start = ((f32[16,1,8,4096]{3,2,1,0:T(8,128)}), f32[16,1,8,4096]{3,2,1,0:T(8,128)S(1)}, u32[]{:S(2)}, u32[]{:S(2)}) async-start(f32[16,1,8,4096]{3,2,1,0:T(8,128)} %bitcast_dynamic-update-slice_fusion), calls=%async_computation | async-start | bytes 4194304 | tf_op jit(solution)/shard_map/all_to_all | solution.py:94
  149.6 0.7 reduce.2
  150.3 0.1 reshape.355
  150.5 0.7 reduce.4
  151.1 0.1 reshape.353
  151.5 0.1 copy.80
  151.6 45.4 %all-to-all-done = f32[16,1,8,4096]{3,2,1,0:T(8,128)S(1)} async-done(((f32[16,1,8,4096]{3,2,1,0:T(8,128)}), f32[16,1,8,4096]{3,2,1,0:T(8,128)S(1)}, u32[]{:S(2)}, u32[]{:S(2)}) %all-to-all-start) | async-done | bytes 2097184 | tf_op jit(solution)/shard_map/all_to_all | solution.py:94
  197.0 0.7 fusion.1
  197.8 0.7 fusion.7
  (27 shorter events, 0.5 us)
Async XLA Ops:
  6.5 55.4 %copy-start = (bf16[8,2048]{1,0:T(8,128)(2,1)S(1)}, bf16[8,2048]{1,0:T(8,128)(2,1)}, u32[]{:S(2)}) copy-start(bf16[8,2048]{1,0:T(8,128)(2,1)} %param.9) | copy-start | bytes 98308
  6.5 41.0 %all-gather.2.cloned.1.call-start = ((), (), s32[]{:S(2)}) async-start(), calls=%async_computation.3 | async-start | bytes 1114112 | tf_op jit(solution)/shard_map/all_gather | solution.py:40
  8.6 3.7 %copy-start.2 = (bf16[512,2048]{1,0:T(8,128)(2,1)S(1)}, bf16[512,2048]{1,0:T(8,128)(2,1)}, u32[]{:S(2)}) copy-start(bf16[512,2048]{1,0:T(8,128)(2,1)} %param.11) | copy-start | bytes 6291460
  14.8 34.3 %copy-start.5 = (bf16[8,2048]{1,0:T(8,128)(2,1)S(1)}, bf16[8,2048]{1,0:T(8,128)(2,1)}, u32[]{:S(2)}) copy-start(bf16[8,2048]{1,0:T(8,128)(2,1)} %param.8) | copy-start | bytes 98308
  14.8 34.6 %copy-start.4 = (bf16[64,8,16,128]{3,2,1,0:T(8,128)(2,1)S(1)}, bf16[64,8,16,128]{3,2,1,0:T(8,128)(2,1)}, u32[]{:S(2)}) copy-start(bf16[64,8,16,128]{3,2,1,0:T(8,128)(2,1)} %copy.112) | copy-start | bytes 6291460
  51.0 3.2 %copy-start.1 = (f32[16,512,128,2]{2,1,3,0:T(8,128)}, f32[16,512,128,2]{2,1,3,0:T(8,128)S(1)}, u32[]{:S(2)}) copy-start(f32[16,512,128,2]{2,1,3,0:T(8,128)S(1)} %get-tuple-element.63) | copy-start | bytes 25165828
  54.3 8.1 %copy-start.3 = (bf16[512,2048]{0,1:T(8,128)(2,1)S(1)}, bf16[512,2048]{0,1:T(8,128)(2,1)}, u32[]{:S(2)}) copy-start(bf16[512,2048]{0,1:T(8,128)(2,1)} %copy.94) | copy-start | bytes 6291460
  56.5 76.9 %all-to-all-start.2 = ((f32[16,1,256]{2,1,0:T(1,128)}), f32[16,1,256]{2,1,0:T(1,128)S(1)}, u32[]{:S(2)}, u32[]{:S(2)}) async-start(f32[16,1,256]{2,1,0:T(1,128)} %reshape.354), calls=%async_computation.2 | async-start | bytes 32768 | tf_op jit(solution)/shard_map/all_to_all | solution.py:103
  133.4 10.2 %all-to-all-start.1 = ((f32[16,1,256]{2,1,0:T(1,128)}), f32[16,1,256]{2,1,0:T(1,128)S(1)}, u32[]{:S(2)}, u32[]{:S(2)}) async-start(f32[16,1,256]{2,1,0:T(1,128)} %reshape.352), calls=%async_computation.1 | async-start | bytes 32768 | tf_op jit(solution)/shard_map/all_to_all | solution.py:102
  143.6 53.4 %all-to-all-start = ((f32[16,1,8,4096]{3,2,1,0:T(8,128)}), f32[16,1,8,4096]{3,2,1,0:T(8,128)S(1)}, u32[]{:S(2)}, u32[]{:S(2)}) async-start(f32[16,1,8,4096]{3,2,1,0:T(8,128)} %bitcast_dynamic-update-slice_fusion), calls=%async_computation | async-start | bytes 4194304 | tf_op jit(solution)/shard_map/all_to_all | solution.py:94
Sparse Core Ops, SparseCore 0:
  9.5 38.0 all-gather.1
